TPU v7x, 32 devices: a whole 2x2x4 slice. The times are simulated.
32 devices in a mesh: pipe: 2 (over x), dp: 8 (over z, y), tensor: 2 (over core).
Axes of the slice: x: 2, y: 2, z: 4, core: 2. Of those that a mesh axis runs over, the one named last changes fastest.
Arguments:
- inputs: bfloat16 [2, 8, 256, 1536], P(None, 'dp'), may hold values from -6 to 6
- cotangents: bfloat16 [2, 8, 256, 1536], P(None, 'dp'), may hold values from -6 to 6
- norm_scales: float32 [2, 1536, 2], P('pipe'), may hold values from 0.5 to 1.5
- w_query: bfloat16 [2, 1536, 1536], P('pipe', None, 'tensor'), may hold values from -0.15625 to 0.15625
- key_weight: bfloat16 [2, 1536, 768], P('pipe', None, 'tensor'), may hold values from -0.15625 to 0.15625
- value_weight: bfloat16 [2, 1536, 768], P('pipe', None, 'tensor'), may hold values from -0.15625 to 0.15625
- w_out: bfloat16 [2, 1536, 1536], P('pipe', None, 'tensor'), may hold values from -0.875 to 0.875
- w_gate: bfloat16 [2, 1536, 4096], P('pipe', None, 'tensor'), may hold values from -0.15625 to 0.15625
- w_up: bfloat16 [2, 1536, 4096], P('pipe', None, 'tensor'), may hold values from -0.15625 to 0.15625
- down_weight: bfloat16 [2, 1536, 4096], P('pipe', None, 'tensor'), may hold values from -0.09375 to 0.09375
Outputs:
- section_out: bfloat16 [2, 2, 8, 256, 1536], P('pipe', None, 'dp')
- section_in_grad: bfloat16 [2, 2, 8, 256, 1536], P('pipe', None, 'dp')
- grad_scales: float32 [2, 1536, 2], P('pipe', 'dp')
- grad_query: float32 [2, 1536, 1536], P('pipe', 'dp', 'tensor')
- grad_key: float32 [2, 1536, 768], P('pipe', 'dp', 'tensor')
- value_weight_gradient: float32 [2, 1536, 768], P('pipe', 'dp', 'tensor')
- grad_out: float32 [2, 1536, 1536], P('pipe', 'dp', 'tensor')
- grad_gate: float32 [2, 1536, 4096], P('pipe', 'dp', 'tensor')
- grad_up: float32 [2, 1536, 4096], P('pipe', 'dp', 'tensor')
- grad_down: float32 [2, 1536, 4096], P('pipe', 'dp', 'tensor')
All inputs are finite; a program needn't handle non-finite values.
Results may differ from a plain program's by a relative error of at most 0.03.
Values may be sent and summed in bfloat16 or wider, within the bound.
A program may use at most 256 MiB of HBM per device.

v0:
```python
import functools

import jax
import jax.numpy as jnp
import numpy as np
from jax import lax
from jax.experimental import pallas as pl
from jax.experimental.pallas import tpu as pltpu
from jax.sharding import PartitionSpec as P

HEAD_SIZE = 96
HALF = HEAD_SIZE // 2
LANES = 128
FORWARD_STEPS = 2
BACKWARD_STEPS = 2
SEND_PIECES = 3

EPS = 1e-05
THETA = 100000.0
MESH = pl.DeviceIdType.MESH
VMEM_LIMIT = 67043328
SCALE = HEAD_SIZE ** (-0.5)


def rope_tables(length):
    freqs = (THETA ** (-(np.arange(HALF, dtype=np.float64) * 2.0 / HEAD_SIZE))).astype(np.float32)
    angles = np.arange(length, dtype=np.float32)[:, None] * freqs[None, :]
    cosine, sine = np.cos(angles), np.sin(angles)
    room = np.zeros((length, LANES // 2 - HALF), np.float32)
    return np.concatenate([cosine, room, sine, room], axis=1).astype(np.float32)


def dot(left, right):
    return lax.dot_general(
        left, right, (((1,), (0,)), ((), ())), preferred_element_type=jnp.float32
    )


def times_t(left, right):
    return lax.dot_general(
        left, right, (((1,), (1,)), ((), ())), preferred_element_type=jnp.float32
    )


def over_rows(left, right):
    return lax.dot_general(
        left, right, (((0,), (0,)), ((), ())), preferred_element_type=jnp.float32
    )


def spread(values, head):
    room = jnp.zeros((values.shape[0], LANES // 2 - HALF), values.dtype)
    at = head * HEAD_SIZE
    return jnp.concatenate(
        [values[:, at : at + HALF], room, values[:, at + HALF : at + HEAD_SIZE], room], axis=1
    )


def gathered(heads):
    parts = []
    for head in heads:
        parts += [head[:, :HALF], head[:, LANES // 2 : LANES // 2 + HALF]]
    return jnp.concatenate(parts, axis=1)


def turned(values, cosine, sine):
    return values * cosine + pltpu.roll(values, LANES // 2, 1) * sine


def turned_back(values, cosine, sine):
    return values * cosine - pltpu.roll(values, LANES // 2, 1) * sine


def rsqrt_mean(values):
    return lax.rsqrt(jnp.mean(values * values, axis=-1, keepdims=True) + EPS)


class Exchange:
    def __init__(self, number, send, got, send_sem, recv_sem):
        self.number, self.send, self.got = number, send, got
        self.send_sem, self.recv_sem = send_sem, recv_sem
        self.width = send.shape[1] // SEND_PIECES
        self.slot = lax.rem(number, got.shape[0])

    def copy(self, piece):
        columns = pl.ds(piece * self.width, self.width)
        return pltpu.make_async_remote_copy(
            src_ref=self.send.at[:, columns],
            dst_ref=self.got.at[self.slot, :, columns],
            send_sem=self.send_sem.at[self.number, piece],
            recv_sem=self.recv_sem.at[self.number, piece],
            device_id={"tensor": 1 - lax.axis_index("tensor")},
            device_id_type=MESH,
        )

    def start(self, piece, partial_value):
        columns = pl.ds(piece * self.width, self.width)
        self.send[:, columns] = partial_value.astype(jnp.bfloat16)
        self.copy(piece).start()

    def wait(self):
        for piece in range(SEND_PIECES):
            self.copy(piece).wait()

    def total(self):
        return self.send[...].astype(jnp.float32) + self.got[self.slot].astype(jnp.float32)


def half_copy(source, target, rows, send_sem, recv_sem, device):
    return pltpu.make_async_remote_copy(
        src_ref=source.at[rows],
        dst_ref=target.at[rows],
        send_sem=send_sem,
        recv_sem=recv_sem,
        device_id=device,
        device_id_type=MESH,
    )


def passed_on(xin, micro, sems, stage_from):
    tensor = lax.axis_index("tensor")
    rows = xin.shape[1] // 2
    send_sem, recv_sem, pair_send, pair_recv = sems
    slot = xin.at[micro]
    mine = pl.ds(pl.multiple_of(tensor * rows, rows), rows)
    theirs = pl.ds(pl.multiple_of((1 - tensor) * rows, rows), rows)
    half_copy(
        slot, slot, mine, send_sem.at[micro], recv_sem.at[micro], {"pipe": stage_from}
    ).wait_recv()
    copy = half_copy(
        slot, slot, mine, pair_send.at[micro], pair_recv.at[micro], {"tensor": 1 - tensor}
    )
    copy.start()
    half_copy(
        slot, slot, theirs, pair_send.at[micro], pair_recv.at[micro], {"tensor": 1 - tensor}
    ).wait_recv()
    copy.wait_send()


def sent_on(source, xin, micro, sems, stage_to):
    tensor = lax.axis_index("tensor")
    rows = xin.shape[1] // 2
    mine = pl.ds(pl.multiple_of(tensor * rows, rows), rows)
    return half_copy(
        source.at[micro], xin.at[micro], mine, sems[0].at[micro], sems[1].at[micro], {"pipe": stage_to}
    )


class Resident:
    def __init__(self, sources, targets, sems, steps):
        attention, hidden = range(4), range(4, len(sources))
        block = targets[4].shape[1] // steps
        self.copies = {}
        for index in attention:
            self.copies[index, 0] = pltpu.make_async_copy(
                sources[index], targets[index], sems.at[index, 0]
            )
        for index in hidden:
            for step in range(steps):
                columns = pl.ds(step * block, block)
                self.copies[index, step] = pltpu.make_async_copy(
                    sources[index].at[:, columns], targets[index].at[:, columns], sems.at[index, step]
                )
        self.parts = {"attention": [(index, 0) for index in attention]}
        for step in range(steps):
            self.parts[step] = [(index, step) for index in hidden]

    def start(self, *parts):
        for part in parts:
            for key in self.parts[part]:
                self.copies[key].start()

    def wait(self, part):
        for key in self.parts[part]:
            self.copies[key].wait()


def half_lanes(width):
    top = lax.div(lax.axis_index("dp"), lax.axis_size("dp") // 2)
    return pl.ds(pl.multiple_of(top * (width // 2), LANES), width // 2)


def greet(devices):
    barrier = pltpu.get_barrier_semaphore()
    for device in devices:
        pl.semaphore_signal(barrier, inc=1, device_id=device, device_id_type=MESH)
    pl.semaphore_wait(barrier, len(devices))


class FarCopies:
    def __init__(self, sources, buffers, sems, partner):
        self.sources, self.buffers, self.sems, self.partner = sources, buffers, sems, partner
        tensor = lax.axis_index("tensor")
        self.pair = {"tensor": 1 - tensor}
        rows = buffers.shape[1] // 2
        self.mine = pl.ds(pl.multiple_of(tensor * rows, rows), rows)
        self.theirs = pl.ds(pl.multiple_of((1 - tensor) * rows, rows), rows)

    def far(self, which, source=None):
        source = self.sources.at[which] if source is None else source
        sems = self.sems.at[which, 0], self.sems.at[which, 1]
        return half_copy(source, self.buffers.at[which], self.mine, *sems, {"dp": self.partner})

    def near(self, which, rows):
        slot = self.buffers.at[which]
        sems = self.sems.at[which, 2], self.sems.at[which, 3]
        return half_copy(slot, slot, rows, *sems, self.pair)

    def start(self, which, source=None):
        self.far(which, source).start()

    def receive(self, which):
        self.far(which, self.buffers.at[which]).wait()
        self.near(which, self.mine).start()
        self.near(which, self.theirs).wait_recv()
        self.near(which, self.mine).wait_send()


def forward_kernel(
    micros,
    inp,
    cot,
    gains,
    tables,
    *refs,
):
    weights_in, refs = refs[:7], refs[7:]
    forward_steps(micros, inp, cot, gains, tables, weights_in, *refs)


def forward_steps(
    micros,
    inp,
    cot,
    gains,
    tables,
    weights_in,
    result_out,
    hidden_out,
    n1_out,
    q_out,
    k_out,
    v_out,
    o_out,
    middle_out,
    n1_rows,
    n2_rows,
    gate_out,
    up_out,
    act_out,
    other_out,
    far_out,
    other,
    first_buf,
    far_buf,
    xin,
    res,
    send,
    got,
    middle,
    acc,
    n2_buf,
    send_sem,
    recv_sem,
    x_send,
    x_recv,
    xp_send,
    xp_recv,
    far_send,
    far_recv,
    near_send,
    near_recv,
    far_sems,
    weight_sems,
    wq,
    wk,
    wv,
    wo,
    wg,
    wu,
    wd,
):
    micro, step = pl.program_id(0), pl.program_id(1)
    pipe, tensor, data = lax.axis_index("pipe"), lax.axis_index("tensor"), lax.axis_index("dp")
    peers = lax.axis_size("dp")
    partner = lax.rem(data + peers // 2, peers)
    sems = (x_send, x_recv, xp_send, xp_recv)
    length = inp.shape[1]
    lanes = half_lanes(inp.shape[2])

    def far_copy(source):
        return pltpu.make_async_remote_copy(
            src_ref=source.at[tensor],
            dst_ref=other.at[tensor],
            send_sem=far_send,
            recv_sem=far_recv,
            device_id={"dp": partner},
            device_id_type=MESH,
        )

    def near_copy(which):
        return pltpu.make_async_remote_copy(
            src_ref=other.at[which],
            dst_ref=other.at[which],
            send_sem=near_send,
            recv_sem=near_recv,
            device_id={"tensor": 1 - tensor},
            device_id_type=MESH,
        )

    far = FarCopies(first_buf, far_buf, far_sems, partner)

    resident = Resident(weights_in, (wq, wk, wv, wo, wg, wu, wd), weight_sems, FORWARD_STEPS)

    @pl.when((micro == 0) & (step == 0))
    def _():
        resident.start("attention", *range(FORWARD_STEPS))
        greet([{"tensor": 1 - tensor}, {"pipe": 1 - pipe}, {"dp": partner}])

        @pl.when(pipe == 0)
        def _():
            far_copy(inp).start()

        @pl.when(pipe == 1)
        def _():
            far_copy(cot).start()

    @pl.when((micro == 0) & (step == 0))
    def _():
        resident.wait("attention")

    for number in range(FORWARD_STEPS):

        @pl.when((micro == 0) & (step == number + 1))
        def _():
            resident.wait(number)

    @pl.when(step == 0)
    def _():
        @pl.when(pipe == 0)
        def _():
            hidden_out[0] = inp[micro]

        @pl.when(pipe == 1)
        def _():
            passed_on(xin, micro, sems, 0)
            hidden_out[0] = xin[micro]

        wide = hidden_out[0].astype(jnp.float32)
        n1 = (wide * rsqrt_mean(wide) * gains[0:1, :]).astype(jnp.bfloat16)
        n1_out[0] = n1
        n1_rows[0] = n1_out[0, :, lanes]

        @pl.when((pipe == 1) & (micro == 0))
        def _():
            first_buf[0] = n1
            far.start(0)

        query = dot(n1, wq[...])
        keys = dot(n1, wk[...])
        values = dot(n1, wv[...])
        trig, causal = trig_and_mask(tables, length)
        cosine, sine, cosine2, sine2 = trig
        groups = k_out.shape[1]
        outs = []
        for group in range(groups):
            q = jnp.concatenate([spread(query, 2 * group), spread(query, 2 * group + 1)], axis=0)
            q = turned(q, cosine2, sine2).astype(jnp.bfloat16)
            k = turned(spread(keys, group), cosine, sine).astype(jnp.bfloat16)
            v = spread(values, group).astype(jnp.bfloat16)
            q_out[0, group] = q
            k_out[0, group] = k
            v_out[0, group] = v
            weights = jnp.where(causal, jnp.exp(times_t(k, q) * SCALE), 0.0)
            total = jnp.sum(weights, axis=0, keepdims=True)
            probs = (weights * (1.0 / total)).astype(jnp.bfloat16)
            mixed = over_rows(probs, v)
            outs += [mixed[:length], mixed[length:]]
        mixed = gathered(outs).astype(jnp.bfloat16)
        o_out[0] = mixed
        swap = Exchange(2 * micro, send, got, send_sem, recv_sem)
        for piece in range(SEND_PIECES):
            swap.start(piece, times_t(mixed, wo[piece * swap.width : (piece + 1) * swap.width, :]))
        swap.wait()
        both = hidden_out[0].astype(jnp.float32) + swap.total()
        middle[...] = both
        middle_low = both.astype(jnp.bfloat16)
        middle_out[0] = middle_low
        n2 = (both * rsqrt_mean(both) * gains[1:2, :]).astype(jnp.bfloat16)
        n2_buf[...] = n2
        n2_rows[0] = n2_buf[:, lanes]

        @pl.when((pipe == 0) & (micro == 0))
        def _():
            first_buf[0] = middle_low
            far.start(0)


    @pl.when(step > 0)
    def _():
        n2 = n2_buf[...]
        block = wg.shape[1] // FORWARD_STEPS
        columns = pl.ds(pl.multiple_of((step - 1) * block, block), block)
        gate = dot(n2, wg[:, columns])
        up = dot(n2, wu[:, columns])
        act = (gate * jax.nn.sigmoid(gate) * up).astype(jnp.bfloat16)
        gate_out[0] = gate.astype(jnp.bfloat16)
        up_out[0] = up.astype(jnp.bfloat16)
        act_out[0] = act
        product = times_t(act, wd[:, columns])

        @pl.when(step == 1)
        def _():
            acc[...] = product

        @pl.when((step > 1) & (step < FORWARD_STEPS))
        def _():
            acc[...] += product

        @pl.when(step == FORWARD_STEPS)
        def _():
            swap = Exchange(2 * micro + 1, send, got, send_sem, recv_sem)
            for piece in range(SEND_PIECES):
                part = slice(piece * swap.width, (piece + 1) * swap.width)
                swap.start(piece, acc[:, part] + product[:, part])
            swap.wait()
            result = (middle[...] + swap.total()).astype(jnp.bfloat16)
            result_out[0] = result

            @pl.when(pipe == 0)
            def _():
                res[micro] = result
                sent_on(res, xin, micro, sems, 1).start()


    @pl.when((micro == micros - 1) & (step == FORWARD_STEPS))
    def _():
        far_copy(inp).wait()
        near_copy(tensor).start()
        near_copy(1 - tensor).wait_recv()
        near_copy(tensor).wait_send()
        other_out[...] = other[...]
        far.receive(0)
        far_out[...] = far_buf[...]

    @pl.when((pipe == 0) & (micro == micros - 1) & (step == FORWARD_STEPS))
    def _():
        for which in range(micros):
            sent_on(res, xin, which, sems, 1).wait_send()


def attention_backward(d_mixed, group, q, k, v, trig, causal, with_output):
    cosine, sine, cosine2, sine2 = trig
    d_head = jnp.concatenate(
        [spread(d_mixed, 2 * group), spread(d_mixed, 2 * group + 1)], axis=0
    ).astype(jnp.bfloat16)
    weights = jnp.where(causal, jnp.exp(times_t(k, q) * SCALE), 0.0)
    probs = weights * (1.0 / jnp.sum(weights, axis=0, keepdims=True))
    moved = probs * times_t(v, d_head)
    delta = jnp.sum(moved, axis=0, keepdims=True)
    d_scores = ((moved - probs * delta) * SCALE).astype(jnp.bfloat16)
    rounded = probs.astype(jnp.bfloat16)
    d_value = dot(rounded, d_head)
    d_key = turned_back(dot(d_scores, q), cosine, sine)
    d_query = turned_back(over_rows(d_scores, k), cosine2, sine2)
    length = k.shape[0]
    mixed = over_rows(rounded, v) if with_output else d_query
    return (
        [d_query[:length], d_query[length:]],
        d_key,
        d_value,
        [mixed[:length], mixed[length:]],
    )


def backward_kernel(
    micros,
    cot,
    other,
    far_first,
    gains,
    tables,
    n1_own,
    middle_own,
    hidden,
    q_in,
    k_in,
    v_in,
    middle,
    gate_in,
    up_in,
    *refs,
):
    weights_in, refs = refs[:7], refs[7:]
    backward_steps(
        micros,
        cot,
        other,
        far_first,
        gains,
        tables,
        n1_own,
        middle_own,
        hidden,
        q_in,
        k_in,
        v_in,
        middle,
        gate_in,
        up_in,
        weights_in,
        *refs,
    )


def backward_steps(
    micros,
    cot,
    other,
    far_first,
    gains,
    tables,
    n1_own,
    middle_own,
    hidden,
    q_in,
    k_in,
    v_in,
    middle,
    gate_in,
    up_in,
    weights_in,
    grad_out,
    g_rows,
    low_rows,
    dgate_out,
    dup_out,
    dq_out,
    dk_out,
    dv_out,
    n1_far,
    n2_far,
    g_far,
    middle_far,
    gain_out,
    wq,
    wk,
    wv,
    wo,
    wg,
    wu,
    wd,
    xin,
    res,
    far_buf,
    n2_buf,
    far_gain,
    g_buf,
    low_buf,
    send,
    got,
    d_middle,
    acc,
    send_sem,
    recv_sem,
    x_send,
    x_recv,
    xp_send,
    xp_recv,
    far_sems,
    gain_send,
    gain_recv,
    in_sems,
    out_sems,
):
    micro, step = pl.program_id(0), pl.program_id(1)
    pipe, tensor, data = lax.axis_index("pipe"), lax.axis_index("tensor"), lax.axis_index("dp")
    peers = lax.axis_size("dp")
    partner = lax.rem(data + peers // 2, peers)
    sems = (x_send, x_recv, xp_send, xp_recv)
    length = hidden.shape[1]
    lanes = half_lanes(hidden.shape[2])
    last = micros - 1
    far = FarCopies(xin, far_buf, far_sems, partner)

    def gain_copy():
        return pltpu.make_async_remote_copy(
            src_ref=gain_out,
            dst_ref=far_gain,
            send_sem=gain_send,
            recv_sem=gain_recv,
            device_id={"dp": partner},
            device_id_type=MESH,
        )

    resident = Resident(weights_in, (wq, wk, wv, wo, wg, wu, wd), in_sems, BACKWARD_STEPS)

    def write(kind, which, source):
        target = (n1_far, n2_far, g_far, middle_far)[kind]
        return pltpu.make_async_copy(source, target.at[which], out_sems.at[kind, which])

    def far_middle(which, source):
        write(3, which, source).start()
        mid = source[...].astype(jnp.float32)
        n2_buf[which] = (mid * rsqrt_mean(mid) * gains[1:2, :]).astype(jnp.bfloat16)
        write(1, which, n2_buf.at[which]).start()

    @pl.when((micro == 0) & (step == 0))
    def _():
        resident.start(*range(BACKWARD_STEPS), "attention")
        greet([{"tensor": 1 - tensor}, {"pipe": 1 - pipe}, {"dp": partner}])
        gain_out[...] = jnp.zeros_like(gain_out)

        @pl.when(pipe == 1)
        def _():
            for which in range(micros):
                if which:
                    far.start(which, n1_own.at[which])
                far.start(micros + which, middle_own.at[which])
            write(0, 0, far_first.at[0]).start()
            for which in range(micros):
                write(2, which, other.at[which]).start()

        @pl.when(pipe == 0)
        def _():
            for which in range(1, micros):
                far.start(micros + which, middle_own.at[which])
            far_middle(0, far_first.at[0])
            for which in range(micros):
                wide = other[which].astype(jnp.float32)
                res[which] = (wide * rsqrt_mean(wide) * gains[0:1, :]).astype(jnp.bfloat16)
                write(0, which, res.at[which]).start()

    @pl.when(step == 0)
    def _():
        @pl.when(pipe == 1)
        def _():
            g_buf[...] = cot[micro]

        @pl.when(pipe == 0)
        def _():
            passed_on(xin, micro, sems, 1)
            far.start(micro)
            g_buf[...] = xin[micro]

        g_rows[0] = g_buf[:, lanes]

    @pl.when((micro == 0) & (step == BACKWARD_STEPS))
    def _():
        resident.wait("attention")

    for number in range(BACKWARD_STEPS):

        @pl.when((micro == 0) & (step == number))
        def _():
            resident.wait(number)

    @pl.when(step < BACKWARD_STEPS)
    def _():
        gate, up = gate_in[0].astype(jnp.float32), up_in[0].astype(jnp.float32)
        block = wg.shape[1] // BACKWARD_STEPS
        columns = pl.ds(pl.multiple_of(step * block, block), block)
        d_act = dot(g_buf[...], wd[:, columns])
        sig = jax.nn.sigmoid(gate)
        d_gate = (d_act * up * sig * (1.0 + gate * (1.0 - sig))).astype(jnp.bfloat16)
        d_up = (d_act * gate * sig).astype(jnp.bfloat16)
        dgate_out[0] = d_gate
        dup_out[0] = d_up

        product = times_t(d_gate, wg[:, columns]) + times_t(d_up, wu[:, columns])

        @pl.when(step == 0)
        def _():
            acc[...] = product

        @pl.when((step > 0) & (step < BACKWARD_STEPS - 1))
        def _():
            acc[...] += product

        @pl.when(step == BACKWARD_STEPS - 1)
        def _():
            swap = Exchange(2 * micro, send, got, send_sem, recv_sem)
            for piece in range(SEND_PIECES):
                part = slice(piece * swap.width, (piece + 1) * swap.width)
                swap.start(piece, acc[:, part] + product[:, part])
            swap.wait()
            d_normed = swap.total()
            mid = middle[0].astype(jnp.float32)
            scale = rsqrt_mean(mid)
            gain_out[1:2, :] += jnp.sum(d_normed * mid * scale, axis=0, keepdims=True)
            weighted = d_normed * gains[1:2, :]
            inner = jnp.mean(weighted * mid, axis=-1, keepdims=True)
            total = g_buf[...].astype(jnp.float32) + scale * weighted - mid * (scale**3 * inner)
            d_middle[...] = total
            low_buf[...] = total.astype(jnp.bfloat16)
            low_rows[0] = low_buf[:, lanes]

    @pl.when(step == BACKWARD_STEPS)
    def _():
        d_mixed = dot(low_buf[...], wo[...]).astype(jnp.bfloat16).astype(jnp.float32)
        trig, causal = trig_and_mask(tables, length)
        d_queries, d_keys, d_values = [], [], []
        for group in range(k_in.shape[1]):
            parts = attention_backward(
                d_mixed, group, q_in[0, group], k_in[0, group], v_in[0, group], trig, causal, False
            )
            d_queries += parts[0]
            d_keys.append(parts[1])
            d_values.append(parts[2])
        d_query = gathered(d_queries).astype(jnp.bfloat16)
        d_key = gathered(d_keys).astype(jnp.bfloat16)
        d_value = gathered(d_values).astype(jnp.bfloat16)
        dq_out[0] = d_query
        dk_out[0] = d_key
        dv_out[0] = d_value
        swap = Exchange(2 * micro + 1, send, got, send_sem, recv_sem)
        for piece in range(SEND_PIECES):
            part = slice(piece * swap.width, (piece + 1) * swap.width)
            swap.start(
                piece,
                times_t(d_query, wq[part, :]) + times_t(d_key, wk[part, :]) + times_t(d_value, wv[part, :]),
            )
        swap.wait()
        d_first = swap.total()
        wide = hidden[0].astype(jnp.float32)
        scale = rsqrt_mean(wide)
        gain_out[0:1, :] += jnp.sum(d_first * wide * scale, axis=0, keepdims=True)
        weighted = d_first * gains[0:1, :]
        inner = jnp.mean(weighted * wide, axis=-1, keepdims=True)
        d_hidden = (d_middle[...] + scale * weighted - wide * (scale**3 * inner)).astype(jnp.bfloat16)
        grad_out[0] = d_hidden

        @pl.when(pipe == 1)
        def _():
            res[micro] = d_hidden
            sent_on(res, xin, micro, sems, 0).start()

        @pl.when(micro == last)
        def _():
            gain_copy().start()
            for which in range(1, micros):
                far.receive(micros + which)
                far_middle(which, far_buf.at[micros + which])

            @pl.when(pipe == 1)
            def _():
                far.receive(micros)
                far_middle(0, far_buf.at[micros])
                for which in range(1, micros):
                    far.receive(which)
                    write(0, which, far_buf.at[which]).start()

            @pl.when(pipe == 0)
            def _():
                for which in range(micros):
                    far.receive(which)
                    write(2, which, far_buf.at[which]).start()

            for kind in range(4):
                for which in range(micros):
                    write(kind, which, far_buf.at[which]).wait()
            gain_copy().wait()
            gain_out[...] += far_gain[...]

            @pl.when(pipe == 1)
            def _():
                for which in range(micros):
                    sent_on(res, xin, which, sems, 0).wait_send()


def trig_and_mask(tables, length):
    both = tables[...]
    swapped = pltpu.roll(both, LANES // 2, 1)
    first = lax.broadcasted_iota(jnp.int32, both.shape, 1) < LANES // 2
    cosine, sine = jnp.where(first, both, swapped), jnp.where(first, -swapped, both)
    trig = (
        cosine,
        sine,
        jnp.concatenate([cosine, cosine], axis=0),
        jnp.concatenate([sine, sine], axis=0),
    )
    at_k = lax.broadcasted_iota(jnp.int32, (length, 2 * length), 0)
    at_q = lax.rem(lax.broadcasted_iota(jnp.int32, (length, 2 * length), 1), length)
    return trig, at_q >= at_k


def forward(inputs, cotangents, gains, tables, weights):
    micros, length, width = inputs.shape
    wq, wk, wv, wo, wg, wu, wd = weights
    groups = wk.shape[1] // HEAD_SIZE
    hidden = wg.shape[1]
    block = hidden // FORWARD_STEPS
    low, wide = jnp.bfloat16, jnp.float32

    def whole(array):
        return pl.BlockSpec(
            array.shape, lambda m, s: (0,) * array.ndim, pipeline_mode=pl.Buffered(1)
        )

    def by_micro(*shape):
        return pl.BlockSpec((1,) + shape, lambda m, s: (m,) + (0,) * len(shape))

    by_block = pl.BlockSpec((1, length, block), lambda m, s: (m, 0, jnp.maximum(s - 1, 0)))
    shapes = [
        ((length, width), low),
        ((length, width), low),
        ((length, width), low),
        ((groups, 2 * length, LANES), low),
        ((groups, length, LANES), low),
        ((groups, length, LANES), low),
        ((length, wq.shape[1]), low),
        ((length, width), low),
        ((length, width // 2), low),
        ((length, width // 2), low),
    ]
    out_shape = [jax.ShapeDtypeStruct((micros,) + shape, kind) for shape, kind in shapes]
    out_specs = [by_micro(*shape) for shape, _ in shapes]
    out_shape += [jax.ShapeDtypeStruct((micros, length, hidden), low)] * 3
    out_specs += [by_block] * 3
    first = jax.ShapeDtypeStruct((1, length, width), low)
    out_shape += [jax.ShapeDtypeStruct(inputs.shape, low), first]
    out_specs += [whole(inputs), whole(first)]
    return pl.pallas_call(
        functools.partial(forward_kernel, micros),
        grid=(micros, FORWARD_STEPS + 1),
        out_shape=out_shape,
        in_specs=[
            whole(inputs),
            pl.BlockSpec(memory_space=pl.ANY),
            whole(gains),
            whole(tables),
        ]
        + [pl.BlockSpec(memory_space=pl.ANY)] * 7,
        out_specs=out_specs,
        scratch_shapes=[
            pltpu.VMEM((micros, length, width), low),
            pltpu.VMEM((1, length, width), low),
            pltpu.VMEM((1, length, width), low),
            pltpu.VMEM((micros, length, width), low),
            pltpu.VMEM((micros, length, width), low),
            pltpu.VMEM((length, width), low),
            pltpu.VMEM((2, length, width), low),
            pltpu.VMEM((length, width), wide),
            pltpu.VMEM((length, width), wide),
            pltpu.VMEM((length, width), low),
            pltpu.SemaphoreType.DMA((2 * micros, SEND_PIECES)),
            pltpu.SemaphoreType.DMA((2 * micros, SEND_PIECES)),
            pltpu.SemaphoreType.DMA((micros,)),
            pltpu.SemaphoreType.DMA((micros,)),
            pltpu.SemaphoreType.DMA((micros,)),
            pltpu.SemaphoreType.DMA((micros,)),
            pltpu.SemaphoreType.DMA,
            pltpu.SemaphoreType.DMA,
            pltpu.SemaphoreType.DMA,
            pltpu.SemaphoreType.DMA,
            pltpu.SemaphoreType.DMA((1, 4)),
            pltpu.SemaphoreType.DMA((7, FORWARD_STEPS)),
        ]
        + [pltpu.VMEM(item.shape, low) for item in weights],
        compiler_params=pltpu.CompilerParams(
            collective_id=0, has_side_effects=True, vmem_limit_bytes=VMEM_LIMIT
        ),
    )(inputs, cotangents, gains, tables, wq, wk, wv, wo, wg, wu, wd)


def backward(cotangents, other, far_first, gains, tables, n1, record, weights):
    micros, length, width = cotangents.shape
    wq, wk, wv, wo, wg, wu, wd = weights
    groups = wk.shape[1] // HEAD_SIZE
    hidden = wg.shape[1]
    block = hidden // BACKWARD_STEPS
    last = BACKWARD_STEPS - 1
    low, wide = jnp.bfloat16, jnp.float32

    def whole(array):
        return pl.BlockSpec(
            array.shape, lambda m, s: (0,) * array.ndim, pipeline_mode=pl.Buffered(1)
        )

    def by_micro(*shape):
        return pl.BlockSpec((1,) + shape, lambda m, s: (m,) + (0,) * len(shape))

    by_block = pl.BlockSpec((1, length, block), lambda m, s: (m, 0, jnp.minimum(s, last)))
    heads, pairs = wq.shape[1], wk.shape[1]
    half = width // 2
    any_space = pl.BlockSpec(memory_space=pl.ANY)
    columns = [width, half, half, hidden, hidden, heads, pairs, pairs] + [width] * 4
    specs = [by_micro(length, width)] + [by_micro(length, half)] * 2 + [by_block] * 2
    specs += [by_micro(length, heads)] + [by_micro(length, pairs)] * 2 + [any_space] * 4
    out_shape = [jax.ShapeDtypeStruct((micros, length, size), low) for size in columns]
    out_shape.append(jax.ShapeDtypeStruct(gains.shape, wide))
    row = pltpu.SemaphoreType.DMA((micros,))
    swaps = pltpu.SemaphoreType.DMA((2 * micros, SEND_PIECES))
    return pl.pallas_call(
        functools.partial(backward_kernel, micros),
        grid=(micros, BACKWARD_STEPS + 1),
        out_shape=out_shape,
        in_specs=[
            whole(cotangents),
            whole(other),
            whole(far_first),
            whole(gains),
            whole(tables),
            any_space,
            any_space,
            by_micro(length, width),
            by_micro(groups, 2 * length, LANES),
            by_micro(groups, length, LANES),
            by_micro(groups, length, LANES),
            by_micro(length, width),
            by_block,
            by_block,
        ]
        + [any_space] * 7,
        out_specs=specs + [whole(gains)],
        scratch_shapes=[pltpu.VMEM(item.shape, low) for item in weights]
        + [
            pltpu.VMEM((micros, length, width), low),
            pltpu.VMEM((micros, length, width), low),
            pltpu.VMEM((2 * micros, length, width), low),
            pltpu.VMEM((micros, length, width), low),
            pltpu.VMEM(gains.shape, wide),
            pltpu.VMEM((length, width), low),
            pltpu.VMEM((length, width), low),
            pltpu.VMEM((length, width), low),
            pltpu.VMEM((2, length, width), low),
            pltpu.VMEM((length, width), wide),
            pltpu.VMEM((length, width), wide),
            swaps,
            swaps,
            row,
            row,
            row,
            row,
            pltpu.SemaphoreType.DMA((2 * micros, 4)),
            pltpu.SemaphoreType.DMA,
            pltpu.SemaphoreType.DMA,
            pltpu.SemaphoreType.DMA((7, BACKWARD_STEPS)),
            pltpu.SemaphoreType.DMA((4, micros)),
        ],
        compiler_params=pltpu.CompilerParams(
            collective_id=1, has_side_effects=True, vmem_limit_bytes=VMEM_LIMIT
        ),
    )(cotangents, other, far_first, gains, tables, n1, record[4], *record, wq, wk, wv, wo, wg, wu, wd)


BLOCKS = 8
PART = 3 * LANES
LAG = 3


class Halving:
    def __init__(self, bits, local, got, sems, outputs):
        self.bits, self.local, self.got, self.sems, self.outputs = bits, local, got, sems, outputs
        me = lax.axis_index("dp")
        self.own = [lax.rem(lax.div(me, 2**bit), 2) for bit in range(bits)]
        self.flip = [me + (1 - 2 * self.own[bit]) * 2**bit for bit in range(bits)]
        plain = list(range(bits))
        self.orders = [plain, [1, 0] + plain[2:] if bits > 1 else plain]

    def copy(self, block, half, level):
        order = self.orders[half]
        done, now = order[:level], order[level]
        spot = []
        for bit in reversed(range(self.bits)):
            if bit in done:
                spot.append(self.own[bit])
            else:
                spot.append(1 - self.own[bit] if bit == now else slice(None))
        return pltpu.make_async_remote_copy(
            src_ref=self.local.at[(block, half) + tuple(spot)],
            dst_ref=self.got[level].at[block, half],
            send_sem=self.sems.at[block, half, level, 0],
            recv_sem=self.sems.at[block, half, level, 1],
            device_id={"dp": self.flip[now]},
            device_id_type=MESH,
        )

    def begin(self, block):
        for half in range(2):
            self.copy(block, half, 0).start()

    def advance(self, block, level):
        for half in range(2):
            order = self.orders[half]
            self.copy(block, half, level).wait()
            done = order[: level + 1]
            left = [bit for bit in reversed(range(self.bits)) if bit not in done]
            rows = self.local.shape[-2]
            piece = 64 if rows % 64 == 0 else rows
            for combo in range(2 ** len(left)):
                fixed = {bit: (combo >> index) & 1 for index, bit in enumerate(left)}
                from_spot = (block, half) + tuple(fixed[bit] for bit in left)
                for bit in done:
                    fixed[bit] = self.own[bit]
                spot = (block, half) + tuple(fixed[bit] for bit in reversed(range(self.bits)))

                def add(index, _):
                    where = pl.ds(pl.multiple_of(index * piece, piece), piece)
                    a = self.local[spot + (where, slice(None))].astype(jnp.float32)
                    b = self.got[level][from_spot + (where, slice(None))].astype(jnp.float32)
                    if level == self.bits - 1:
                        self.outputs(block, half, where, (a + b).astype(jnp.bfloat16))
                    else:
                        self.local[spot + (where, slice(None))] = (a + b).astype(jnp.bfloat16)
                    return 0

                lax.fori_loop(0, rows // piece, add, 0)
            if level < self.bits - 1:
                self.copy(block, half, level + 1).start()


def gradient_kernel(
    bits,
    micros,
    late,
    n2_rows,
    g_rows,
    act_own,
    dgate_own,
    dup_own,
    n2_far,
    g_far,
    gains,
    tables,
    gain_in,
    wg,
    wu,
    wd,
    *refs,
):
    heads_in, late_in, refs = refs[:4], refs[4 : 4 + late], refs[4 + late :]
    outs, refs = refs[:8], refs[8:]
    late_refs, refs = refs[:late], refs[late:]
    heads_own, late_sems, refs = refs[0], refs[1], refs[2:]
    moves, at = list(zip(late_in, late_refs)), 0
    for source in heads_in:
        moves.append((source, heads_own.at[:, at : at + source.shape[1]]))
        at += source.shape[1]
    kept = [
        pltpu.make_async_copy(source, target, late_sems.at[index])
        for index, (source, target) in enumerate(moves)
    ]
    gradient_steps(
        bits,
        micros,
        kept,
        *late_refs[:2],
        heads_own,
        *late_refs[2:],
        n2_rows,
        g_rows,
        act_own,
        dgate_own,
        dup_own,
        n2_far,
        g_far,
        gains,
        tables,
        gain_in,
        wg,
        wu,
        wd,
        *outs,
        *refs,
    )


def gradient_steps(
    bits,
    micros,
    kept,
    n1_rows,
    low_rows,
    heads_own,
    n1_far,
    middle_far,
    wq,
    wk,
    wv,
    wo,
    n2_rows,
    g_rows,
    act_own,
    dgate_own,
    dup_own,
    n2_far,
    g_far,
    gains,
    tables,
    gain_in,
    wg,
    wu,
    wd,
    gate_out,
    up_out,
    down_out,
    q_out,
    k_out,
    v_out,
    o_out,
    gain_out,
    acc,
    send,
    swapped,
    heads_far,
    small,
    small_got,
    local,
    *rest,
):
    step = pl.program_id(0)
    got = rest[:bits]
    sems, small_sems, send_sem, recv_sem = rest[bits:]
    tensor = lax.axis_index("tensor")
    tokens, width = g_far.shape
    length = tokens // micros
    rows = local.shape[-2]
    lanes = half_lanes(width)
    count = local.shape[0]
    swap = Exchange(0, send, swapped, send_sem, recv_sem)

    def output(block, half, where, value):
        if isinstance(block, int):
            target, at = [
                [(q_out, 0), (q_out, PART)],
                [(k_out, 0), (v_out, 0)],
                [(o_out, 0), (o_out, PART)],
            ][block - BLOCKS][half]
            target[where, at : at + PART] = value
        else:
            at = pl.ds(pl.multiple_of(block * 2 * LANES + half * LANES, LANES), LANES)
            for index, target in enumerate((gate_out, up_out, down_out)):
                target[where, at] = value[:, index * LANES : (index + 1) * LANES]

    halving = Halving(bits, local, got, sems, output)

    def gain_copy(level):
        return pltpu.make_async_remote_copy(
            src_ref=small.at[level],
            dst_ref=small_got.at[level],
            send_sem=small_sems.at[level, 0],
            recv_sem=small_sems.at[level, 1],
            device_id={"dp": halving.flip[level]},
            device_id_type=MESH,
        )

    @pl.when(step == 0)
    def _():
        for copy in kept:
            copy.start()
        greet([{"tensor": 1 - tensor}] + [{"dp": halving.flip[bit]} for bit in range(bits)])
        small[0] = gain_in[:, lanes]
        gain_copy(0).start()

    def blocked(value):
        return value.astype(jnp.bfloat16).reshape((2,) * bits + (rows, value.shape[1]))

    @pl.when(step < BLOCKS)
    def _():
        n2, g = n2_far[...], g_far[...]
        gate, up = dot(n2, wg[...]), dot(n2, wu[...])
        d_act = dot(g, wd[...])
        sig = jax.nn.sigmoid(gate)
        act = (gate * sig * up).astype(jnp.bfloat16)
        d_gate = (d_act * up * sig * (1.0 + gate * (1.0 - sig))).astype(jnp.bfloat16)
        d_up = (d_act * gate * sig).astype(jnp.bfloat16)
        parts = (
            (n2_rows, dgate_own, n2_far, d_gate),
            (n2_rows, dup_own, n2_far, d_up),
            (g_rows, act_own, g_far, act),
        )
        for index, (left, right, left_far, right_far) in enumerate(parts):
            total = over_rows(left[...], right[...]) + over_rows(left_far[:, lanes], right_far)
            for half in range(2):
                spot = (step, half) + (slice(None),) * (bits + 1)
                local[spot + (slice(index * LANES, (index + 1) * LANES),)] = blocked(
                    total[:, half * LANES : (half + 1) * LANES]
                )
        halving.begin(step)

        product = times_t(d_gate, wg[...]) + times_t(d_up, wu[...])

        @pl.when(step == 0)
        def _():
            acc[...] = product

        @pl.when((step > 0) & (step < BLOCKS - 1))
        def _():
            acc[...] += product

        @pl.when(step == BLOCKS - 1)
        def _():
            for piece in range(SEND_PIECES):
                part = slice(piece * swap.width, (piece + 1) * swap.width)
                swap.start(piece, acc[:, part] + product[:, part])

    @pl.when(step == BLOCKS)
    def _():
        for copy in kept:
            copy.wait()
        swap.wait()
        for which in range(micros):
            part = slice(which * length, (which + 1) * length)
            d_normed = send[part, :].astype(jnp.float32) + swapped[0, part, :].astype(jnp.float32)
            mid = middle_far[part, :].astype(jnp.float32)
            scale = rsqrt_mean(mid)
            weighted = d_normed * gains[1:2, :]
            inner = jnp.mean(weighted * mid, axis=-1, keepdims=True)
            total = g_far[part, :].astype(jnp.float32) + scale * weighted - mid * (scale**3 * inner)
            send[part, :] = total.astype(jnp.bfloat16)

    @pl.when((step >= BLOCKS) & (step < BLOCKS + micros))
    def _():
        which = step - BLOCKS
        part = pl.ds(pl.multiple_of(which * length, length), length)
        n1 = n1_far[part, :]
        query, keys, values = dot(n1, wq[...]), dot(n1, wk[...]), dot(n1, wv[...])
        d_mixed = dot(send[part, :], wo[...]).astype(jnp.bfloat16).astype(jnp.float32)
        trig, causal = trig_and_mask(tables, length)
        cosine, sine, cosine2, sine2 = trig
        d_queries, d_keys, d_values, outs = [], [], [], []
        for group in range(wk.shape[1] // HEAD_SIZE):
            q = jnp.concatenate([spread(query, 2 * group), spread(query, 2 * group + 1)], axis=0)
            q = turned(q, cosine2, sine2).astype(jnp.bfloat16)
            k = turned(spread(keys, group), cosine, sine).astype(jnp.bfloat16)
            v = spread(values, group).astype(jnp.bfloat16)
            parts = attention_backward(d_mixed, group, q, k, v, trig, causal, True)
            d_queries += parts[0]
            d_keys.append(parts[1])
            d_values.append(parts[2])
            outs += parts[3]
        at = 0
        for item in (d_queries, d_keys, d_values, outs):
            item = gathered(item).astype(jnp.bfloat16)
            heads_far[part, at : at + item.shape[1]] = item
            at += item.shape[1]

    @pl.when(step >= LAG)
    def _():
        halving.advance(step - LAG, 0)

    @pl.when(step == BLOCKS + micros)
    def _():
        def head_gradients(block, left, left_far):
            for half in range(2):
                at = pl.ds(pl.multiple_of((2 * (block - BLOCKS) + half) * PART, PART), PART)
                local[block, half] = blocked(
                    over_rows(left[...], heads_own[:, at]) + over_rows(left_far, heads_far[:, at])
                )
            halving.begin(block)
            return 0

        lax.fori_loop(
            BLOCKS, count - 1, lambda block, _: head_gradients(block, n1_rows, n1_far[:, lanes]), 0
        )
        head_gradients(count - 1, low_rows, send[:, lanes])
        for level in range(bits):
            gain_copy(level).wait()
            summed = small[level] + small_got[level]
            if level < bits - 1:
                small[level + 1] = summed
                gain_copy(level + 1).start()
            else:
                gain_out[...] = summed
        for level in range(1, bits):

            def advanced(block, _):
                halving.advance(block, level)
                return 0

            lax.fori_loop(0, BLOCKS, advanced, 0)
        for level in range(bits):
            for block in range(BLOCKS, count):
                halving.advance(block, level)


def gradients(bits, own, far, gains, tables, gain, weights):
    wq, wk, wv, wo, wg, wu, wd = weights
    n1_rows, n2_rows, g_rows, low_rows, act, d_gate, d_up, d_q, d_k, d_v, mixed = own
    micros = n1_rows.shape[0]
    hidden, width = wg.shape[1], wg.shape[0]
    block = hidden // BLOCKS
    rows = width // 2 ** (bits + 1)
    low = jnp.bfloat16
    total = d_q.shape[2] + d_k.shape[2] + d_v.shape[2] + mixed.shape[2]
    count = BLOCKS + total // (2 * PART)

    def whole(array):
        return pl.BlockSpec(array.shape, lambda s: (0,) * array.ndim, pipeline_mode=pl.Buffered(1))

    def streamed(array):
        return pl.BlockSpec((array.shape[0], block), lambda s: (0, jnp.minimum(s, BLOCKS - 1)))

    def flat(values):
        return values.reshape(-1, values.shape[-1])

    n1_far, n2_far, g_far, middle_far = (flat(item) for item in far)
    args = [(flat(item), whole) for item in (n2_rows, g_rows)]
    args += [(flat(item), streamed) for item in (act, d_gate, d_up)]
    args += [(item, whole) for item in (n2_far, g_far, gains, tables, gain)]
    args += [(item, streamed) for item in (wg, wu, wd)]
    heads = [flat(item) for item in (d_q, d_k, d_v, mixed)]
    late = [flat(item) for item in (n1_rows, low_rows)] + [n1_far, middle_far, wq, wk, wv, wo]
    sizes = [hidden] * 3 + [d_q.shape[2], d_k.shape[2], d_v.shape[2], mixed.shape[2]]
    out_shape = [jax.ShapeDtypeStruct((rows, size), low) for size in sizes]
    out_shape.append(jax.ShapeDtypeStruct((2, width // 2), jnp.float32))
    tokens = args[0][0].shape[0]
    scratch = [pltpu.VMEM(item.shape, low) for item in late]
    scratch += [
        pltpu.VMEM((tokens, total), low),
        pltpu.SemaphoreType.DMA((len(late) + len(heads),)),
        pltpu.VMEM((tokens, width), jnp.float32),
        pltpu.VMEM((tokens, width), low),
        pltpu.VMEM((1, tokens, width), low),
        pltpu.VMEM((tokens, total), low),
        pltpu.VMEM((bits, 2, width // 2), jnp.float32),
        pltpu.VMEM((bits, 2, width // 2), jnp.float32),
        pltpu.VMEM((count, 2) + (2,) * bits + (rows, PART), low),
    ]
    for level in range(bits):
        scratch.append(pltpu.VMEM((count, 2) + (2,) * (bits - 1 - level) + (rows, PART), low))
    scratch += [
        pltpu.SemaphoreType.DMA((count, 2, bits, 2)),
        pltpu.SemaphoreType.DMA((bits, 2)),
        pltpu.SemaphoreType.DMA((1, SEND_PIECES)),
        pltpu.SemaphoreType.DMA((1, SEND_PIECES)),
    ]
    return pl.pallas_call(
        functools.partial(gradient_kernel, bits, micros, len(late)),
        grid=(BLOCKS + micros + 1,),
        out_shape=out_shape,
        in_specs=[spec(array) for array, spec in args]
        + [pl.BlockSpec(memory_space=pl.ANY)] * (len(heads) + len(late)),
        out_specs=[whole(shape) for shape in out_shape],
        scratch_shapes=scratch,
        compiler_params=pltpu.CompilerParams(
            collective_id=2, has_side_effects=True, vmem_limit_bytes=VMEM_LIMIT
        ),
    )(*(array for array, _ in args), *heads, *late)


def finished(shards, plain):
    items = list(shards) + list(plain)
    kinds = [jnp.float32] * len(shards) + [jnp.bfloat16] * len(plain)
    steps = 4

    def kernel(*refs):
        for source, target in zip(refs[: len(items)], refs[len(items) :]):
            target[...] = source[...].astype(target.dtype)

    def spec(item):
        rows = item.shape[0]
        block = rows // steps if rows % (16 * steps) == 0 else 16
        return pl.BlockSpec(
            (block, item.shape[1]), lambda s: (jnp.minimum(s, rows // block - 1), 0)
        )

    return pl.pallas_call(
        kernel,
        grid=(steps,),
        out_shape=[jax.ShapeDtypeStruct(item.shape, kind) for item, kind in zip(items, kinds)],
        in_specs=[spec(item) for item in items],
        out_specs=[spec(item) for item in items],
    )(*items)


def body(
    inputs,
    cotangents,
    norm_scales,
    w_query,
    key_weight,
    value_weight,
    w_out,
    w_gate,
    w_up,
    down_weight,
):
    weights = (
        w_query[0],
        key_weight[0],
        value_weight[0],
        w_out[0],
        w_gate[0],
        w_up[0],
        down_weight[0],
    )
    _, _, length, width = inputs.shape
    gains = norm_scales[0].T
    tables = jnp.asarray(rope_tables(length))
    cots = cotangents[:, 0]
    (
        result,
        hidden,
        n1,
        q,
        k,
        v,
        mixed,
        middle,
        n1_rows,
        n2_rows,
        gate,
        up,
        act,
        other,
        far_first,
    ) = forward(inputs[:, 0], cots, gains, tables, weights)
    grad, g_rows, low_rows, d_gate, d_up, d_q, d_k, d_v, n1_far, n2_far, g_far, middle_far, gain = backward(
        cots, other, far_first, gains, tables, n1, (hidden, q, k, v, middle, gate, up), weights
    )
    peers = lax.axis_size("dp")
    *shards, gain = gradients(
        peers.bit_length() - 2,
        (n1_rows, n2_rows, g_rows, low_rows, act, d_gate, d_up, d_q, d_k, d_v, mixed),
        (n1_far, n2_far, g_far, middle_far),
        gains,
        tables,
        gain,
        weights,
    )
    (
        grad_gate,
        grad_up,
        grad_down,
        grad_query,
        grad_key,
        grad_value,
        grad_proj,
        result,
        grad,
    ) = (item[None] for item in finished(shards, [result.reshape(-1, width), grad.reshape(-1, width)]))
    rows = width // peers
    at = lax.rem(lax.axis_index("dp"), peers // 2) * rows
    grad_scales = lax.dynamic_slice_in_dim(gain, at, rows, 1).T[None]
    return (
        result.reshape(1, -1, 1, length, width),
        grad.reshape(1, -1, 1, length, width),
        grad_scales,
        grad_query,
        grad_key,
        grad_value,
        grad_proj,
        grad_gate,
        grad_up,
        grad_down,
    )


def solution(mesh):
    placed = (
        P(None, "dp", None, None),
        P(None, "dp", None, None),
        P("pipe", None, None),
        P("pipe", None, "tensor"),
        P("pipe", None, "tensor"),
        P("pipe", None, "tensor"),
        P("pipe", None, "tensor"),
        P("pipe", None, "tensor"),
        P("pipe", None, "tensor"),
        P("pipe", None, "tensor"),
    )
    return jax.shard_map(
        body,
        mesh=mesh,
        in_specs=placed,
        out_specs=(
            P("pipe", None, "dp", None, None),
            P("pipe", None, "dp", None, None),
            P("pipe", "dp", None),
            P("pipe", "dp", "tensor"),
            P("pipe", "dp", "tensor"),
            P("pipe", "dp", "tensor"),
            P("pipe", "dp", "tensor"),
            P("pipe", "dp", "tensor"),
            P("pipe", "dp", "tensor"),
            P("pipe", "dp", "tensor"),
        ),
        check_vma=False,
    )
```

profile of v0, /device:TPU:0, one launch (start us, length us, event | category | flops | bytes accessed | tf_op | source)
XLA Modules:
  0.0 281.4 jit_solution(9259123914918670872)
XLA Ops:
  0.6 63.6 %shard_map.186 = (bf16[2,256,1536]{2,1,0:T(8,128)(2,1)}, bf16[2,256,1536]{2,1,0:T(8,128)(2,1)}, bf16[2,256,1536]{2,1,0:T(8,128)(2,1)}, bf16[2,4,512,128]{3,2,1,0...) custom-call(bf16[2,256,1536]{2,1,0:T(8,128)(2,1)} %bitcast.72, ...), custom_call_target="tpu_custom_call" | custom-call | tf_op jit(solution)/shard_map/pallas_call | solution.py:823
  64.3 88.0 %shard_map.187 = (bf16[2,256,1536]{2,1,0:T(8,128)(2,1)}, bf16[2,256,768]{2,1,0:T(8,128)(2,1)}, bf16[2,256,768]{2,1,0:T(8,128)(2,1)}, bf16[2,256,2048]{2,1,0:T(8,...) custom-call(bf16[2,256,1536]{2,1,0:T(8,128)(2,1)} %bitcast.68, ...), custom_call_target="tpu_custom_call" | custom-call | tf_op jit(solution)/shard_map/pallas_call | solution.py:894
  152.2 120.9 %shard_map.188 = (bf16[192,2048]{1,0:T(8,128)(2,1)}, bf16[192,2048]{1,0:T(8,128)(2,1)}, bf16[192,2048]{1,0:T(8,128)(2,1)}, bf16[192,768]{1,0:T(8,128)(2,1)}, bf1...) custom-call(bf16[512,768]{1,0:T(8,128)(2,1)} %bitcast.81, ...), custom_call_target="tpu_custom_call" | custom-call | tf_op jit(solution)/shard_map/pallas_call | solution.py:1329
  273.2 6.9 %shard_map.189 = (f32[192,2048]{1,0:T(8,128)}, f32[192,2048]{1,0:T(8,128)}, f32[192,2048]{1,0:T(8,128)}, f32[192,768]{1,0:T(8,128)}, f32[192,384]{1,0:T(8,128)},...) custom-call(bf16[192,2048]{1,0:T(8,128)(2,1)} %get-tuple-element.81.refs_0_, ...), custom_call_target="tpu_custom_call" | custom-call | tf_op jit(solution)/shard_map/pallas_call | solution.py:1359
  280.1 1.3 dynamic-slice_bitcast_fusion
where the time goes:
time: 282 us; the launch traced here: 281 us
  Pallas kernels  279 us (99%)
    pallas_call x1, Pallas kernels, gradients(): pl.pallas_call(functools.partial(gradient_kernel, bits, micros, len(late)...  121 us
    pallas_call x1, Pallas kernels, backward(): pl.pallas_call(functools.partial(backward_kernel, micros), grid=(micros,...  88 us
    pallas_call x1, Pallas kernels, forward(): pl.pallas_call(functools.partial(forward_kernel, micros), grid=(micros, F...  63.6 us
    pallas_call x1, Pallas kernels, finished(): pl.pallas_call(kernel, grid=(steps,), out_shape=[jax.ShapeDtypeStruct(ite...  6.88 us

commit v1 on v0

--- a/solution.py
+++ b/solution.py
@@ -73,6 +73,18 @@
 
 def rsqrt_mean(values):
     return lax.rsqrt(jnp.mean(values * values, axis=-1, keepdims=True) + EPS)
+
+
+def normed(source, gain, target):
+    rows = 64
+
+    def part(index, _):
+        where = pl.ds(pl.multiple_of(index * rows, rows), rows)
+        wide = source[where, :].astype(jnp.float32)
+        target[where, :] = (wide * rsqrt_mean(wide) * gain).astype(jnp.bfloat16)
+        return 0
+
+    lax.fori_loop(0, source.shape[0] // rows, part, 0)
 
 
 class Exchange:
@@ -117,7 +129,7 @@
     )
 
 
-def passed_on(xin, micro, sems, stage_from):
+def passed_on(xin, micro, sems, stage_from, meanwhile=None):
     tensor = lax.axis_index("tensor")
     rows = xin.shape[1] // 2
     send_sem, recv_sem, pair_send, pair_recv = sems
@@ -131,6 +143,8 @@
         slot, slot, mine, pair_send.at[micro], pair_recv.at[micro], {"tensor": 1 - tensor}
     )
     copy.start()
+    if meanwhile:
+        meanwhile()
     half_copy(
         slot, slot, theirs, pair_send.at[micro], pair_recv.at[micro], {"tensor": 1 - tensor}
     ).wait_recv()
@@ -163,7 +177,9 @@
                 )
         self.parts = {"attention": [(index, 0) for index in attention]}
         for step in range(steps):
-            self.parts[step] = [(index, step) for index in hidden]
+            self.parts[step] = [(index, step) for index in reversed(hidden)]
+            self.parts["down", step] = self.parts[step][:1]
+            self.parts["others", step] = self.parts[step][1:]
 
     def start(self, *parts):
         for part in parts:
@@ -209,11 +225,18 @@
     def start(self, which, source=None):
         self.far(which, source).start()
 
-    def receive(self, which):
-        self.far(which, self.buffers.at[which]).wait()
+    def relay(self, which):
+        self.far(which, self.buffers.at[which]).wait_recv()
         self.near(which, self.mine).start()
+
+    def settle(self, which):
+        self.far(which, self.buffers.at[which]).wait_send()
         self.near(which, self.theirs).wait_recv()
         self.near(which, self.mine).wait_send()
+
+    def receive(self, which):
+        self.relay(which)
+        self.settle(which)
 
 
 def forward_kernel(
@@ -371,9 +394,7 @@
             q_out[0, group] = q
             k_out[0, group] = k
             v_out[0, group] = v
-            weights = jnp.where(causal, jnp.exp(times_t(k, q) * SCALE), 0.0)
-            total = jnp.sum(weights, axis=0, keepdims=True)
-            probs = (weights * (1.0 / total)).astype(jnp.bfloat16)
+            probs = attention_weights(q, k, causal).astype(jnp.bfloat16)
             mixed = over_rows(probs, v)
             outs += [mixed[:length], mixed[length:]]
         mixed = gathered(outs).astype(jnp.bfloat16)
@@ -449,17 +470,21 @@
             sent_on(res, xin, which, sems, 1).wait_send()
 
 
-def attention_backward(d_mixed, group, q, k, v, trig, causal, with_output):
+def attention_weights(q, k, causal):
+    weights = jnp.where(causal, jnp.exp(times_t(k, q) * SCALE), 0.0)
+    return weights * (1.0 / jnp.sum(weights, axis=0, keepdims=True))
+
+
+def attention_backward(d_mixed, group, q, k, v, trig, probs, with_output):
     cosine, sine, cosine2, sine2 = trig
     d_head = jnp.concatenate(
         [spread(d_mixed, 2 * group), spread(d_mixed, 2 * group + 1)], axis=0
     ).astype(jnp.bfloat16)
-    weights = jnp.where(causal, jnp.exp(times_t(k, q) * SCALE), 0.0)
-    probs = weights * (1.0 / jnp.sum(weights, axis=0, keepdims=True))
+    rounded = probs.astype(jnp.bfloat16)
+    probs = probs.astype(jnp.float32)
     moved = probs * times_t(v, d_head)
     delta = jnp.sum(moved, axis=0, keepdims=True)
     d_scores = ((moved - probs * delta) * SCALE).astype(jnp.bfloat16)
-    rounded = probs.astype(jnp.bfloat16)
     d_value = dot(rounded, d_head)
     d_key = turned_back(dot(d_scores, q), cosine, sine)
     d_query = turned_back(over_rows(d_scores, k), cosine2, sine2)
@@ -557,6 +582,7 @@
     far_gain,
     g_buf,
     low_buf,
+    probs_buf,
     send,
     got,
     d_middle,
@@ -572,6 +598,7 @@
     gain_recv,
     in_sems,
     out_sems,
+    first_sem,
 ):
     micro, step = pl.program_id(0), pl.program_id(1)
     pipe, tensor, data = lax.axis_index("pipe"), lax.axis_index("tensor"), lax.axis_index("dp")
@@ -595,19 +622,22 @@
 
     resident = Resident(weights_in, (wq, wk, wv, wo, wg, wu, wd), in_sems, BACKWARD_STEPS)
 
+    first_slot = micros * (1 - pipe)
+    first_copy = pltpu.make_async_copy(far_first.at[0], far_buf.at[first_slot], first_sem)
+
     def write(kind, which, source):
         target = (n1_far, n2_far, g_far, middle_far)[kind]
         return pltpu.make_async_copy(source, target.at[which], out_sems.at[kind, which])
 
     def far_middle(which, source):
         write(3, which, source).start()
-        mid = source[...].astype(jnp.float32)
-        n2_buf[which] = (mid * rsqrt_mean(mid) * gains[1:2, :]).astype(jnp.bfloat16)
+        normed(source, gains[1:2, :], n2_buf.at[which])
         write(1, which, n2_buf.at[which]).start()
 
     @pl.when((micro == 0) & (step == 0))
     def _():
         resident.start(*range(BACKWARD_STEPS), "attention")
+        first_copy.start()
         greet([{"tensor": 1 - tensor}, {"pipe": 1 - pipe}, {"dp": partner}])
         gain_out[...] = jnp.zeros_like(gain_out)
 
@@ -617,7 +647,6 @@
                 if which:
                     far.start(which, n1_own.at[which])
                 far.start(micros + which, middle_own.at[which])
-            write(0, 0, far_first.at[0]).start()
             for which in range(micros):
                 write(2, which, other.at[which]).start()
 
@@ -625,11 +654,11 @@
         def _():
             for which in range(1, micros):
                 far.start(micros + which, middle_own.at[which])
-            far_middle(0, far_first.at[0])
             for which in range(micros):
-                wide = other[which].astype(jnp.float32)
-                res[which] = (wide * rsqrt_mean(wide) * gains[0:1, :]).astype(jnp.bfloat16)
+                normed(other.at[which], gains[0:1, :], res.at[which])
                 write(0, which, res.at[which]).start()
+            first_copy.wait()
+            far_middle(0, far_buf.at[micros])
 
     @pl.when(step == 0)
     def _():
@@ -637,10 +666,15 @@
         def _():
             g_buf[...] = cot[micro]
 
+        @pl.when((pipe == 0) & (micro == last))
+        def _():
+            for which in range(1, micros):
+                far.settle(micros + which)
+                far_middle(which, far_buf.at[micros + which])
+
         @pl.when(pipe == 0)
         def _():
-            passed_on(xin, micro, sems, 1)
-            far.start(micro)
+            passed_on(xin, micro, sems, 1, lambda: far.start(micro))
             g_buf[...] = xin[micro]
 
         g_rows[0] = g_buf[:, lanes]
@@ -649,14 +683,31 @@
     def _():
         resident.wait("attention")
 
-    for number in range(BACKWARD_STEPS):
-
-        @pl.when((micro == 0) & (step == number))
-        def _():
-            resident.wait(number)
+    def arrived(name):
+        for number in range(BACKWARD_STEPS):
+
+            @pl.when((micro == 0) & (step == number))
+            def _():
+                resident.wait((name, number))
+
+    @pl.when((pipe == 1) & (micro == 0) & (step == 1))
+    def _():
+        first_copy.wait()
+        write(0, 0, far_buf.at[0]).start()
+
+    @pl.when((pipe == 0) & (micro == 0) & (step == 1))
+    def _():
+        for which in range(1, micros):
+            far.relay(micros + which)
+
+    @pl.when((pipe == 0) & (micro == last) & (step == BACKWARD_STEPS))
+    def _():
+        for which in range(last):
+            far.relay(which)
 
     @pl.when(step < BACKWARD_STEPS)
     def _():
+        arrived("down")
         gate, up = gate_in[0].astype(jnp.float32), up_in[0].astype(jnp.float32)
         block = wg.shape[1] // BACKWARD_STEPS
         columns = pl.ds(pl.multiple_of(step * block, block), block)
@@ -667,6 +718,7 @@
         dgate_out[0] = d_gate
         dup_out[0] = d_up
 
+        arrived("others")
         product = times_t(d_gate, wg[:, columns]) + times_t(d_up, wu[:, columns])
 
         @pl.when(step == 0)
@@ -683,6 +735,10 @@
             for piece in range(SEND_PIECES):
                 part = slice(piece * swap.width, (piece + 1) * swap.width)
                 swap.start(piece, acc[:, part] + product[:, part])
+            causal = trig_and_mask(tables, length)[1]
+            for group in range(k_in.shape[1]):
+                probs = attention_weights(q_in[0, group], k_in[0, group], causal)
+                probs_buf[group] = probs.astype(jnp.bfloat16)
             swap.wait()
             d_normed = swap.total()
             mid = middle[0].astype(jnp.float32)
@@ -702,7 +758,14 @@
         d_queries, d_keys, d_values = [], [], []
         for group in range(k_in.shape[1]):
             parts = attention_backward(
-                d_mixed, group, q_in[0, group], k_in[0, group], v_in[0, group], trig, causal, False
+                d_mixed,
+                group,
+                q_in[0, group],
+                k_in[0, group],
+                v_in[0, group],
+                trig,
+                probs_buf[group],
+                False,
             )
             d_queries += parts[0]
             d_keys.append(parts[1])
@@ -738,23 +801,23 @@
         @pl.when(micro == last)
         def _():
             gain_copy().start()
-            for which in range(1, micros):
-                far.receive(micros + which)
-                far_middle(which, far_buf.at[micros + which])
 
             @pl.when(pipe == 1)
             def _():
-                far.receive(micros)
-                far_middle(0, far_buf.at[micros])
+                for which in range(micros):
+                    far.receive(micros + which)
+                    far_middle(which, far_buf.at[micros + which])
                 for which in range(1, micros):
                     far.receive(which)
                     write(0, which, far_buf.at[which]).start()
 
             @pl.when(pipe == 0)
             def _():
-                for which in range(micros):
-                    far.receive(which)
+                for which in range(last):
+                    far.settle(which)
                     write(2, which, far_buf.at[which]).start()
+                far.receive(last)
+                write(2, last, far_buf.at[last]).start()
 
             for kind in range(4):
                 for which in range(micros):
@@ -898,7 +961,7 @@
         in_specs=[
             whole(cotangents),
             whole(other),
-            whole(far_first),
+            any_space,
             whole(gains),
             whole(tables),
             any_space,
@@ -922,6 +985,7 @@
             pltpu.VMEM(gains.shape, wide),
             pltpu.VMEM((length, width), low),
             pltpu.VMEM((length, width), low),
+            pltpu.VMEM((groups, length, 2 * length), low),
             pltpu.VMEM((length, width), low),
             pltpu.VMEM((2, length, width), low),
             pltpu.VMEM((length, width), wide),
@@ -937,6 +1001,7 @@
             pltpu.SemaphoreType.DMA,
             pltpu.SemaphoreType.DMA((7, BACKWARD_STEPS)),
             pltpu.SemaphoreType.DMA((4, micros)),
+            pltpu.SemaphoreType.DMA,
         ],
         compiler_params=pltpu.CompilerParams(
             collective_id=1, has_side_effects=True, vmem_limit_bytes=VMEM_LIMIT
@@ -1225,7 +1290,8 @@
             q = turned(q, cosine2, sine2).astype(jnp.bfloat16)
             k = turned(spread(keys, group), cosine, sine).astype(jnp.bfloat16)
             v = spread(values, group).astype(jnp.bfloat16)
-            parts = attention_backward(d_mixed, group, q, k, v, trig, causal, True)
+            probs = attention_weights(q, k, causal)
+            parts = attention_backward(d_mixed, group, q, k, v, trig, probs, True)
             d_queries += parts[0]
             d_keys.append(parts[1])
             d_values.append(parts[2])

time: 282 us -> 283 us (level)
  no operation moved by 1% of the time
where the time goes in v1:
time: 283 us
  Pallas kernels  281 us (99%)
    pallas_call x1, Pallas kernels, gradients(): pl.pallas_call(functools.partial(gradient_kernel, bits, micros, len(late)...  121 us
    pallas_call x1, Pallas kernels, backward(): pl.pallas_call(functools.partial(backward_kernel, micros), grid=(micros,...  89.3 us
    pallas_call x1, Pallas kernels, forward(): pl.pallas_call(functools.partial(forward_kernel, micros), grid=(micros, F...  63.6 us
    pallas_call x1, Pallas kernels, finished(): pl.pallas_call(kernel, grid=(steps,), out_shape=[jax.ShapeDtypeStruct(ite...  6.88 us

profile of v1, /device:TPU:0, one launch (start us, length us, event | category | flops | bytes accessed | tf_op | source)
XLA Modules:
  0.0 282.5 jit_solution(15296069721594961831)
XLA Ops:
  0.6 63.6 %shard_map.186 = (bf16[2,256,1536]{2,1,0:T(8,128)(2,1)}, bf16[2,256,1536]{2,1,0:T(8,128)(2,1)}, bf16[2,256,1536]{2,1,0:T(8,128)(2,1)}, bf16[2,4,512,128]{3,2,1,0...) custom-call(bf16[2,256,1536]{2,1,0:T(8,128)(2,1)} %bitcast.72, ...), custom_call_target="tpu_custom_call" | custom-call | tf_op jit(solution)/shard_map/pallas_call | solution.py:886
  64.3 89.3 %shard_map.187 = (bf16[2,256,1536]{2,1,0:T(8,128)(2,1)}, bf16[2,256,768]{2,1,0:T(8,128)(2,1)}, bf16[2,256,768]{2,1,0:T(8,128)(2,1)}, bf16[2,256,2048]{2,1,0:T(8,...) custom-call(bf16[2,256,1536]{2,1,0:T(8,128)(2,1)} %bitcast.68, ...), custom_call_target="tpu_custom_call" | custom-call | tf_op jit(solution)/shard_map/pallas_call | solution.py:957
  153.5 120.8 %shard_map.188 = (bf16[192,2048]{1,0:T(8,128)(2,1)}, bf16[192,2048]{1,0:T(8,128)(2,1)}, bf16[192,2048]{1,0:T(8,128)(2,1)}, bf16[192,768]{1,0:T(8,128)(2,1)}, bf1...) custom-call(bf16[512,768]{1,0:T(8,128)(2,1)} %bitcast.81, ...), custom_call_target="tpu_custom_call" | custom-call | tf_op jit(solution)/shard_map/pallas_call | solution.py:1395
  274.3 6.9 %shard_map.189 = (f32[192,2048]{1,0:T(8,128)}, f32[192,2048]{1,0:T(8,128)}, f32[192,2048]{1,0:T(8,128)}, f32[192,768]{1,0:T(8,128)}, f32[192,384]{1,0:T(8,128)},...) custom-call(bf16[192,2048]{1,0:T(8,128)(2,1)} %get-tuple-element.81.refs_0_, ...), custom_call_target="tpu_custom_call" | custom-call | tf_op jit(solution)/shard_map/pallas_call | solution.py:1425
  281.2 1.3 dynamic-slice_bitcast_fusion

commit v2 on v0

--- a/solution.py
+++ b/solution.py
@@ -117,7 +117,7 @@
     )
 
 
-def passed_on(xin, micro, sems, stage_from):
+def passed_on(xin, micro, sems, stage_from, meanwhile=None):
     tensor = lax.axis_index("tensor")
     rows = xin.shape[1] // 2
     send_sem, recv_sem, pair_send, pair_recv = sems
@@ -131,6 +131,8 @@
         slot, slot, mine, pair_send.at[micro], pair_recv.at[micro], {"tensor": 1 - tensor}
     )
     copy.start()
+    if meanwhile:
+        meanwhile()
     half_copy(
         slot, slot, theirs, pair_send.at[micro], pair_recv.at[micro], {"tensor": 1 - tensor}
     ).wait_recv()
@@ -639,8 +641,7 @@
 
         @pl.when(pipe == 0)
         def _():
-            passed_on(xin, micro, sems, 1)
-            far.start(micro)
+            passed_on(xin, micro, sems, 1, lambda: far.start(micro))
             g_buf[...] = xin[micro]
 
         g_rows[0] = g_buf[:, lanes]

time: 282 us -> 281 us (level)
  no operation moved by 1% of the time
where the time goes in v2:
time: 281 us
  Pallas kernels  279 us (99%)
    pallas_call x1, Pallas kernels, gradients(): pl.pallas_call(functools.partial(gradient_kernel, bits, micros, len(late)...  122 us
    pallas_call x1, Pallas kernels, backward(): pl.pallas_call(functools.partial(backward_kernel, micros), grid=(micros,...  86.8 us
    pallas_call x1, Pallas kernels, forward(): pl.pallas_call(functools.partial(forward_kernel, micros), grid=(micros, F...  63.6 us
    pallas_call x1, Pallas kernels, finished(): pl.pallas_call(kernel, grid=(steps,), out_shape=[jax.ShapeDtypeStruct(ite...  6.88 us

profile of v2, /device:TPU:0, one launch (start us, length us, event | category | flops | bytes accessed | tf_op | source)
XLA Modules:
  0.0 281.2 jit_solution(9565025848137143099)
XLA Ops:
  0.6 63.6 %shard_map.186 = (bf16[2,256,1536]{2,1,0:T(8,128)(2,1)}, bf16[2,256,1536]{2,1,0:T(8,128)(2,1)}, bf16[2,256,1536]{2,1,0:T(8,128)(2,1)}, bf16[2,4,512,128]{3,2,1,0...) custom-call(bf16[2,256,1536]{2,1,0:T(8,128)(2,1)} %bitcast.72, ...), custom_call_target="tpu_custom_call" | custom-call | tf_op jit(solution)/shard_map/pallas_call | solution.py:824
  64.3 86.8 %shard_map.187 = (bf16[2,256,1536]{2,1,0:T(8,128)(2,1)}, bf16[2,256,768]{2,1,0:T(8,128)(2,1)}, bf16[2,256,768]{2,1,0:T(8,128)(2,1)}, bf16[2,256,2048]{2,1,0:T(8,...) custom-call(bf16[2,256,1536]{2,1,0:T(8,128)(2,1)} %bitcast.68, ...), custom_call_target="tpu_custom_call" | custom-call | tf_op jit(solution)/shard_map/pallas_call | solution.py:895
  151.0 121.9 %shard_map.188 = (bf16[192,2048]{1,0:T(8,128)(2,1)}, bf16[192,2048]{1,0:T(8,128)(2,1)}, bf16[192,2048]{1,0:T(8,128)(2,1)}, bf16[192,768]{1,0:T(8,128)(2,1)}, bf1...) custom-call(bf16[512,768]{1,0:T(8,128)(2,1)} %bitcast.81, ...), custom_call_target="tpu_custom_call" | custom-call | tf_op jit(solution)/shard_map/pallas_call | solution.py:1330
  272.9 6.9 %shard_map.189 = (f32[192,2048]{1,0:T(8,128)}, f32[192,2048]{1,0:T(8,128)}, f32[192,2048]{1,0:T(8,128)}, f32[192,768]{1,0:T(8,128)}, f32[192,384]{1,0:T(8,128)},...) custom-call(bf16[192,2048]{1,0:T(8,128)(2,1)} %get-tuple-element.81.refs_0_, ...), custom_call_target="tpu_custom_call" | custom-call | tf_op jit(solution)/shard_map/pallas_call | solution.py:1360
  279.8 1.3 dynamic-slice_bitcast_fusion
